TPU v7x, 32 devices: a whole 2x2x4 slice. The times are simulated.
32 devices in a mesh: shard: 8 (over z, y), tp: 4 (over x, core).
Axes of the slice: x: 2, y: 2, z: 4, core: 2. Of those that a mesh axis runs over, the one named last changes fastest.
Arguments:
- weight_query: bfloat16 [12288, 12288], P('shard', 'tp'), may hold values from -0.078125 to 0.078125
- low_query: bfloat16 [12288, 64], P('shard'), may hold values from -0.0546875 to 0.0546875
- high_query: bfloat16 [64, 12288], P(None, 'tp'), may hold values from -0.75 to 0.75
- weight_key: bfloat16 [12288, 12288], P('shard', 'tp'), may hold values from -0.078125 to 0.078125
- low_key: bfloat16 [12288, 64], P('shard'), may hold values from -0.0546875 to 0.0546875
- high_key: bfloat16 [64, 12288], P(None, 'tp'), may hold values from -0.75 to 0.75
- weight_value: bfloat16 [12288, 12288], P('shard', 'tp'), may hold values from -0.078125 to 0.078125
- low_value: bfloat16 [12288, 64], P('shard'), may hold values from -0.0546875 to 0.0546875
- high_value: bfloat16 [64, 12288], P(None, 'tp'), may hold values from -0.75 to 0.75
- norm_train: float32 [12288], P(('shard', 'tp')), may hold values from 0.25 to 1.75
- norm_step: float32 [12288], P(('shard', 'tp')), may hold values from -0.3 to 0.3
Outputs:
- ready_query: bfloat16 [12288, 12288], P(None, ('tp', 'shard'))
- ready_key: bfloat16 [12288, 12288], P(None, ('tp', 'shard'))
- ready_value: bfloat16 [12288, 12288], P(None, ('tp', 'shard'))
- column_query: float32 [12288], P(('tp', 'shard'))
- column_key: float32 [12288], P(('tp', 'shard'))
- column_value: float32 [12288], P(('tp', 'shard'))
- serve_norm: bfloat16 [12288], replicated
All inputs are finite; a program needn't handle non-finite values. Where the computation divides by a largest or mean magnitude, that divisor is 1e-20 or more.
Results may differ from a plain program's by a relative error of at most 0.001.
Values may be sent and summed in bfloat16 or wider, within the bound.
A program may use at most 192 MiB of HBM per device.

v0:
```python
import functools

import jax
import jax.numpy as jnp
from jax import lax
from jax.experimental import pallas as pl
from jax.experimental.pallas import tpu as pltpu
from jax.sharding import PartitionSpec as P

mix_rate = 0.5
MESH = pl.DeviceIdType.MESH
TILE = 256
RAW = 128
CHUNK = 128
SPLIT = 96


def merged(weight, low, high):
    product = jnp.dot(low, high, preferred_element_type=jnp.float32)
    return weight.astype(jnp.float32) + mix_rate * product


def exchange(
    n, parts, depth,
    wq, wk, wv, lq, lk, lv, hq, hk, hv, train, step,
    land_q, land_k, land_v, col, norm,
    wbuf, ltbuf, lbuf, hbuf, part, stat, raw, rawlow, gains,
    load_sem, high_sem, low_sem, gain_sem,
    send_sem, recv_sem, part_send, part_recv, col_send, col_recv,
    raw_send, raw_recv,
    rlow_send, rlow_recv, norm_send, norm_recv, side_send, side_recv,
):
    weights, lows, highs = (wq, wk, wv), (lq, lk, lv), (hq, hk, hv)
    lands = (land_q, land_k, land_v)
    rows, width = wbuf.shape[2], wbuf.shape[3]
    me, side = lax.axis_index("shard"), lax.axis_index("tp")
    half, pairs = n // 2, n // 4
    top, place, odd = me // half, me % half, me % 2
    own = n - 1

    def target(k):
        flip = lax.rem(odd + k % 2, 2)
        if k < half:
            return 2 * (top * (k // 2) + (1 - top) * (n // 2 - 1 - k // 2)) + flip
        j = (k - half) // 2 + 1
        if j < pairs:
            return 2 * (top * pairs + lax.rem(place // 2 + j, pairs)) + flip
        return me if k == own else me + 1 - 2 * odd

    def cols(k):
        return pl.ds(pl.multiple_of(target(k) * width, 128), width)

    def shifted(d):
        return lax.rem(me + d, n)

    order = list(range(n))
    loads = {}
    for m in range(3):
        loads[m] = pltpu.make_async_copy(lows[m], ltbuf.at[m], low_sem.at[m])
        for k in order:
            loads[m, k] = (
                pltpu.make_async_copy(highs[m].at[:, cols(k)], hbuf.at[m, k], high_sem.at[m, k]),
                pltpu.make_async_copy(weights[m].at[:, cols(k)], wbuf.at[m, k], load_sem.at[m, k]),
            )

    def fetch(m):
        loads[m].start()
        for k in order:
            for copy in loads[m, k]:
                copy.start()

    fetch(0)
    gain_loads = [
        pltpu.make_async_copy(source, gains.at[i], gain_sem.at[i]) for i, source in enumerate((train, step))
    ]
    for copy in gain_loads:
        copy.start()

    barrier = pltpu.get_barrier_semaphore()
    for d in range(1, n):
        pl.semaphore_signal(barrier, inc=1, device_id={"shard": shifted(d)}, device_id_type=MESH)
    for j in range(1, parts):
        pl.semaphore_signal(
            barrier, inc=1, device_id={"tp": lax.rem(side + j, parts)}, device_id_type=MESH
        )
    pl.semaphore_wait(barrier, n - 1 + parts - 1)

    def remote(src, dst, send, recv, device):
        copy = pltpu.make_async_remote_copy(
            src_ref=src, dst_ref=dst, send_sem=send, recv_sem=recv,
            device_id=device, device_id_type=MESH,
        )
        copy.start()
        return copy

    def raw_part(p, k, here):
        at = pl.ds(*((0, SPLIT), (SPLIT, RAW - SPLIT))[p])
        return pltpu.make_async_remote_copy(
            src_ref=wv.at[at, cols(k)], dst_ref=raw.at[here, at],
            send_sem=raw_send.at[p, k], recv_sem=raw_recv.at[p, here],
            device_id={"shard": target(k)}, device_id_type=MESH,
        )

    def raw_low(k, here):
        return pltpu.make_async_remote_copy(
            src_ref=lv.at[:, pl.ds(0, RAW)], dst_ref=rawlow.at[here],
            send_sem=rlow_send.at[k], recv_sem=rlow_recv.at[here],
            device_id={"shard": target(k)}, device_id_type=MESH,
        )

    for k in range(half):
        raw_part(0, k, place).start()
    def sums(m):
        loads[m].wait()
        lbuf[m] = jnp.transpose(ltbuf[m].astype(jnp.float32)).astype(jnp.bfloat16)
        for k in order:
            for copy in loads[m, k]:
                copy.wait()

            def tile(i, total):
                at = pl.ds(pl.multiple_of(i * TILE, TILE), TILE)
                latest = merged(wbuf[m, k, at, :], lbuf[m, at, :], hbuf[m, k])
                return total + jnp.sum(jnp.abs(latest), axis=0, keepdims=True)

            part[m, k] = lax.fori_loop(0, rows // TILE, tile, jnp.zeros((1, width), jnp.float32))
        for k in range(own):
            part_copy(m, k, me).start()

    def part_copy(m, k, source):
        return pltpu.make_async_remote_copy(
            src_ref=part.at[m, k], dst_ref=stat.at[m, source],
            send_sem=part_send.at[m, k], recv_sem=part_recv.at[m, source],
            device_id={"shard": target(k)}, device_id_type=MESH,
        )

    def columns(m):
        total = part[m, own]
        for d in range(1, n):
            source = shifted(d)
            part_copy(m, 0, source).wait_recv()
            total = total + stat[m, source]
        total = total / depth
        col[m, me] = total
        return [
            remote(col.at[m, me], col.at[m, me], col_send.at[m, d], col_recv.at[m, d], {"shard": shifted(d)})
            for d in range(1, n)
        ]

    def settle(copies):
        for copy in copies:
            copy.wait()

    def block_copy(m, k, first, count, source):
        return pltpu.make_async_remote_copy(
            src_ref=wbuf.at[m, k, pl.ds(first, count)],
            dst_ref=lands[m].at[pl.ds(pl.multiple_of(source * rows + first, 16), count)],
            send_sem=send_sem.at[m, k], recv_sem=recv_sem.at[m, source],
            device_id={"shard": target(k)}, device_id_type=MESH,
        )

    def ready(m, start, stop):
        def chunk(slots, i, carry):
            first = pl.multiple_of(i * CHUNK, CHUNK)
            at = pl.ds(first, CHUNK)
            behind = None
            for k in slots:
                latest = merged(wbuf[m, k, at, :], lbuf[m, at, :], hbuf[m, k])
                narrow = (latest / col[m, target(k)]).astype(jnp.bfloat16)
                if k == own:
                    lands[m][pl.ds(pl.multiple_of(me * rows + first, CHUNK), CHUNK), :] = narrow
                else:
                    wbuf[m, k, at, :] = narrow
                if behind is not None:
                    block_copy(m, behind, first, CHUNK, me).start()
                behind = k
            return carry

        near = list(range(half, own))
        mixed = []
        for k in range(half):
            mixed.append(k)
            mixed.extend(near[k:k + 1])
        begin = max(start, RAW // CHUNK) if m == 2 else start
        lax.fori_loop(start, begin, functools.partial(chunk, near + [own]), 0)
        lax.fori_loop(begin, stop, functools.partial(chunk, mixed + [own]), 0)

    chunks = rows // CHUNK
    early = chunks // 4
    chunks = rows // CHUNK
    early = chunks // 4
    sums(0)
    for k in range(half):
        raw_part(1, k, place).start()
        raw_low(k, place).start()
    fetch(1)
    scales = columns(0)
    settle(scales)
    ready(0, 0, early)
    for copy in gain_loads:
        copy.wait()
    norm[me, side, 0, :] = gains[0] + gains[1]
    sums(1)
    fetch(2)
    norms = [
        remote(norm.at[me, side], norm.at[me, side], norm_send.at[d], norm_recv.at[d], {"shard": shifted(d)})
        for d in range(1, n)
    ]
    ready(0, early, 2 * early)
    scales = columns(1)
    sums(2)
    ready(0, 2 * early, 3 * early)
    later = columns(2)
    ready(0, 3 * early, chunks)
    settle(scales)
    ready(1, 0, chunks)
    settle(later)
    ready(2, 0, chunks)

    for copy in norms:
        copy.wait()
    sides = [
        remote(norm.at[:, side], norm.at[:, side], side_send.at[j], side_recv.at[j], {"tp": lax.rem(side + j, parts)})
        for j in range(1, parts)
    ]

    for i in range(half):
        for p in range(2):
            raw_part(p, 0, i).wait_recv()
        raw_low(0, i).wait_recv()
        low = jnp.transpose(rawlow[i].astype(jnp.float32)).astype(jnp.bfloat16)
        latest = merged(raw[i], low, hbuf[2, own])
        source = (1 - top) * half + i
        land_v[pl.ds(pl.multiple_of(source * rows, RAW), RAW), :] = (latest / col[2, me]).astype(jnp.bfloat16)

    for copy in sides:
        copy.wait()
    for k in range(half):
        for p in range(2):
            raw_part(p, k, place).wait_send()
        raw_low(k, place).wait_send()
    for m in range(3):
        for k in range(own):
            part_copy(m, k, me).wait_send()
            first = RAW if m == 2 and k < half else 0
            block_copy(m, k, first, rows - first, me).wait_send()
        for i in range(half):
            first = RAW if m == 2 else 0
            block_copy(m, 0, first, rows - first, (1 - top) * half + i).wait_recv()
        for d in range(1, half):
            block_copy(m, half, 0, rows, top * half + lax.rem(place + d, half)).wait_recv()


def finish(q_in, k_in, v_in, col, norm, q_out, k_out, v_out, q_col, k_col, v_col, serve, sem):
    copies = [
        pltpu.make_async_copy(source, out, sem.at[m])
        for m, (source, out) in enumerate(((q_in, q_out), (k_in, k_out), (v_in, v_out)))
    ]
    for copy in copies:
        copy.start()
    me = lax.axis_index("shard")
    for m, out in enumerate((q_col, k_col, v_col)):
        out[...] = col[m, me, 0, :]
    n, parts, _, piece = norm.shape
    for s in range(n):
        for t in range(parts):
            serve[pl.ds((s * parts + t) * piece, piece)] = norm[s, t, 0, :].astype(jnp.bfloat16)
    for copy in copies:
        copy.wait()


def kernel_body(
    n, parts,
    weight_query, low_query, high_query,
    weight_key, low_key, high_key,
    weight_value, low_value, high_value,
    norm_train, norm_step,
):
    rows, wide = weight_query.shape
    width, depth = wide // n, rows * n
    rank, piece = low_query.shape[1], norm_train.shape[0]
    anywhere = pl.BlockSpec(memory_space=pl.ANY)
    vmem = pl.BlockSpec(memory_space=pltpu.VMEM)
    land = pltpu.VMEM((depth, width), jnp.bfloat16)
    dma = pltpu.SemaphoreType.DMA
    half = n // 2
    gathered = pl.pallas_call(
        functools.partial(exchange, n, parts, depth),
        out_shape=(
            land, land, land,
            pltpu.VMEM((3, n, 1, width), jnp.float32),
            pltpu.VMEM((n, parts, 1, piece), jnp.float32),
        ),
        in_specs=[anywhere] * 11,
        out_specs=(vmem,) * 5,
        scratch_shapes=[
            pltpu.VMEM((3, n, rows, width), jnp.bfloat16),
            pltpu.VMEM((3, rank, rows), jnp.bfloat16),
            pltpu.VMEM((3, rows, rank), jnp.bfloat16),
            pltpu.VMEM((3, n, rank, width), jnp.bfloat16),
            pltpu.VMEM((3, n, 1, width), jnp.float32),
            pltpu.VMEM((3, n, 1, width), jnp.float32),
            pltpu.VMEM((half, RAW, width), jnp.bfloat16),
            pltpu.VMEM((half, rank, RAW), jnp.bfloat16),
            pltpu.VMEM((2, piece), jnp.float32),
            dma((3, n)), dma((3, n)), dma((3,)), dma((2,)),
            dma((3, n)), dma((3, n)), dma((3, n)), dma((3, n)), dma((3, n)), dma((3, n)),
            dma((2, half)), dma((2, half)), dma((half,)), dma((half,)),
            dma((n,)), dma((n,)), dma((parts,)), dma((parts,)),
        ],
        compiler_params=pltpu.CompilerParams(
            collective_id=0, has_side_effects=True, vmem_limit_bytes=35 * 2**20
        ),
        name="exchange",
    )(
        weight_query, weight_key, weight_value,
        low_query.T, low_key.T, low_value.T,
        high_query, high_key, high_value,
        norm_train, norm_step,
    )
    ready = jax.ShapeDtypeStruct((depth, width), jnp.bfloat16)
    column = jax.ShapeDtypeStruct((width,), jnp.float32)
    return pl.pallas_call(
        finish,
        out_shape=(
            (ready,) * 3 + (column,) * 3
            + (jax.ShapeDtypeStruct((n * parts * piece,), jnp.bfloat16),)
        ),
        in_specs=[anywhere] * 3 + [vmem] * 2,
        out_specs=(anywhere,) * 3 + (vmem,) * 4,
        scratch_shapes=[dma((3,))],
        compiler_params=pltpu.CompilerParams(vmem_limit_bytes=2**20),
        name="finish",
    )(*gathered)


def plain_body(
    weight_query, low_query, high_query,
    weight_key, low_key, high_key,
    weight_value, low_value, high_value,
    norm_train, norm_step,
):
    n = lax.axis_size("shard")
    latest = [
        merged(weight, low, high)
        for weight, low, high in (
            (weight_query, low_query, high_query),
            (weight_key, low_key, high_key),
            (weight_value, low_value, high_value),
        )
    ]
    totals = lax.psum(tuple(jnp.sum(jnp.abs(x), axis=0) for x in latest), "shard")
    place = lax.axis_index("shard")
    readies, columns = [], []
    for x, total in zip(latest, totals):
        column = total / (x.shape[0] * n)
        narrow = (x / column).astype(jnp.bfloat16)
        ready = lax.all_to_all(narrow, "shard", split_axis=1, concat_axis=0, tiled=True)
        readies.append(ready)
        columns.append(lax.dynamic_slice_in_dim(column, place * ready.shape[1], ready.shape[1]))
    serve = (norm_train + norm_step).astype(jnp.bfloat16)
    serve = lax.all_gather(serve, ("shard", "tp"), tiled=True)
    return (*readies, *columns, serve)


def solution(mesh):
    n, parts = mesh.shape["shard"], mesh.shape["tp"]

    def body(*args):
        rows, wide = args[0].shape
        fits = (
            n % 4 == 0
            and wide % (n * 128) == 0
            and rows % TILE == 0
            and rows % CHUNK == 0
            and all(args[i].shape == args[0].shape for i in (3, 6))
            and 6 * rows * wide < 40 * 2**20
        )
        if fits:
            return kernel_body(n, parts, *args)
        return plain_body(*args)

    weight, low, high = P("shard", "tp"), P("shard", None), P(None, "tp")
    norm = P(("shard", "tp"))
    ready, column = P(None, ("tp", "shard")), P(("tp", "shard"))
    return jax.shard_map(
        body,
        mesh=mesh,
        in_specs=(weight, low, high) * 3 + (norm, norm),
        out_specs=(ready,) * 3 + (column,) * 3 + (P(),),
        check_vma=False,
    )
```

profile of v0, /device:TPU:30, one launch (start us, length us, event | category | flops | bytes accessed | tf_op | source)
XLA Modules:
  0.0 628.2 jit_solution(1150960970941504810)
XLA Ops:
  0.6 617.2 %exchange.1 = (bf16[12288,384]{1,0:T(8,128)(2,1)S(1)}, bf16[12288,384]{1,0:T(8,128)(2,1)S(1)}, bf16[12288,384]{1,0:T(8,128)(2,1)S(1)}, f32[3,8,1,384]{3,2,1,0:T(1,128)S(1)}, f32[8,4,1,384]{3,2,1,0:T(1,128)S(1)}) custom-call(bf16[1536,3072]{1,0:T(8,128)(2,1)} %wq.1, bf16[1536,3072]{1,0:T(8,128)(2,1)} %wk.1, bf16[1536,3072]{1,0:T(8,128)(2,1)} %wv.1, ...), custom_call_target="tpu_custom_call" | custom-call | tf_op jit(solution)/shard_map/exchange/pallas_call | solution.py:286
  617.8 10.3 %finish.1 = (bf16[12288,384]{1,0:T(8,128)(2,1)}, bf16[12288,384]{1,0:T(8,128)(2,1)}, bf16[12288,384]{1,0:T(8,128)(2,1)}, f32[384]{0:T(512)}, f32[384]{0:T(512)}, /*index=5*/f32[384]{0:T(512)}, bf16[12288]{0:T(1024)(128)(2,1)}) custom-call(bf16[12288,384]{1,0:T(8,128)(2,1)S(1)} %get-tuple-element.12.q_in, bf16[12288,384]{1,0:T(8,128)(2,1)S(1)} %get-tuple-element.13.k_in, ...), custom_call_target="tpu_custom_call" | custom-call | tf_op jit(solution)/shard_map/finish/pallas_call | solution.py:322
where the time goes:
time: 632 us; the launch traced here: 628 us
  Pallas kernels  628 us (99%)
    pallas_call x1, Pallas kernels, kernel_body(): pl.pallas_call(functools.partial(exchange, n, parts, depth), out_shape=(l...  617 us

commit v1 on v0

v1 whole, which is shorter than its diff:
```python
import functools

import jax
import jax.numpy as jnp
from jax import lax
from jax.experimental import pallas as pl
from jax.experimental.pallas import tpu as pltpu
from jax.sharding import PartitionSpec as P

mix_rate = 0.5
MESH = pl.DeviceIdType.MESH
TILE = 256
CHUNK = 128
RAW_PARTS = (160, 48, 48)
RAW = sum(RAW_PARTS)
EXTRA = 512
PIECES = 4


def merged(weight, low, high):
    product = jnp.dot(low, high, preferred_element_type=jnp.float32)
    return weight.astype(jnp.float32) + mix_rate * product


def places(n):
    me = lax.axis_index("shard")
    half, pairs = n // 2, n // 4
    top, place, odd = me // half, me % half, me % 2

    def target(k):
        flip = lax.rem(odd + k % 2, 2)
        if k < half:
            return 2 * (top * (k // 2) + (1 - top) * (n // 2 - 1 - k // 2)) + flip
        j = (k - half) // 2 + 1
        if j < pairs:
            return 2 * (top * pairs + lax.rem(place // 2 + j, pairs)) + flip
        return me if k == n - 1 else me + 1 - 2 * odd

    return me, half, top, place, target


def interleaved(half, own):
    near = list(range(half, own))
    mixed = []
    for k in range(half):
        mixed.append(k)
        mixed.extend(near[k:k + 1])
    return mixed


def exchange(
    n, parts, depth,
    wq, wk, wv, lq, lk, lv, hq, hk, hv, train, step,
    land_q, land_k, later, head, col, norm,
    wbuf, ltbuf, lbuf, hbuf, part, stat, raw, rawlow, gains,
    load_sem, high_sem, low_sem, gain_sem,
    send_sem, recv_sem, part_send, part_recv, col_send, col_recv,
    raw_send, raw_recv, rlow_send, rlow_recv, spread_send, spread_recv,
    norm_send, norm_recv, side_send, side_recv, extra_send, extra_recv,
):
    weights, lows, highs = (wq, wk, wv), (lq, lk, lv), (hq, hk, hv)
    lands = (land_q, land_k)
    rows, width = later.shape[1], later.shape[2]
    me, half, top, place, target = places(n)
    side = lax.axis_index("tp")
    own = n - 1
    share = rawlow.shape[1] // parts

    def block(m, k):
        return later.at[k] if m == 2 else wbuf.at[m, k]

    def cols(k):
        return pl.ds(pl.multiple_of(target(k) * width, 128), width)

    def shifted(d):
        return lax.rem(me + d, n)

    order = list(range(n))
    loads = {}
    for m in range(3):
        loads[m] = pltpu.make_async_copy(lows[m], ltbuf.at[m], low_sem.at[m])
        for k in order:
            loads[m, k] = (
                pltpu.make_async_copy(highs[m].at[:, cols(k)], hbuf.at[m, k], high_sem.at[m, k]),
                pltpu.make_async_copy(weights[m].at[:, cols(k)], block(m, k), load_sem.at[m, k]),
            )

    def fetch(m):
        loads[m].start()
        for k in order:
            for copy in loads[m, k]:
                copy.start()

    fetch(0)
    gain_loads = [
        pltpu.make_async_copy(source, gains.at[i], gain_sem.at[i]) for i, source in enumerate((train, step))
    ]
    for copy in gain_loads:
        copy.start()

    barrier = pltpu.get_barrier_semaphore()
    for d in range(1, n):
        pl.semaphore_signal(barrier, inc=1, device_id={"shard": shifted(d)}, device_id_type=MESH)
    for j in range(1, parts):
        pl.semaphore_signal(
            barrier, inc=1, device_id={"tp": lax.rem(side + j, parts)}, device_id_type=MESH
        )
    pl.semaphore_wait(barrier, n - 1 + parts - 1)

    def remote(src, dst, send, recv, device):
        return pltpu.make_async_remote_copy(
            src_ref=src, dst_ref=dst, send_sem=send, recv_sem=recv,
            device_id=device, device_id_type=MESH,
        )

    def begun(copies):
        for copy in copies:
            copy.start()
        return copies

    def settle(copies):
        for copy in copies:
            copy.wait()

    def raw_part(p, k, here):
        at = pl.ds(sum(RAW_PARTS[:p]), RAW_PARTS[p])
        return remote(
            wv.at[at, cols(k)], raw.at[here, at], raw_send.at[p, k], raw_recv.at[p, here], {"shard": target(k)}
        )

    def raw_low(k, here):
        mine = pl.ds(pl.multiple_of(side * share, share), share)
        return remote(
            lv.at[mine, pl.ds(0, RAW)], rawlow.at[here, mine], rlow_send.at[k], rlow_recv.at[here],
            {"shard": target(k)},
        )

    def send_raw(p):
        for k in range(half):
            raw_part(p, k, place).start()

    def part_copy(m, k, source):
        return remote(
            part.at[m, k], stat.at[m, source], part_send.at[m, k], part_recv.at[m, source], {"shard": target(k)}
        )

    def sums(m):
        loads[m].wait()
        lbuf[m] = jnp.transpose(ltbuf[m].astype(jnp.float32)).astype(jnp.bfloat16)
        for k in order:
            for copy in loads[m, k]:
                copy.wait()

            def tile(i, total):
                at = pl.ds(pl.multiple_of(i * TILE, TILE), TILE)
                latest = merged(block(m, k)[at, :], lbuf[m, at, :], hbuf[m, k])
                return total + jnp.sum(jnp.abs(latest).reshape(TILE // 8, 8, width), axis=0)

            total = lax.fori_loop(0, rows // TILE, tile, jnp.zeros((8, width), jnp.float32))
            part[m, k] = jnp.sum(total, axis=0, keepdims=True)
        for k in range(own):
            part_copy(m, k, me).start()

    def columns(m):
        total = part[m, own]
        for d in range(1, n):
            source = shifted(d)
            part_copy(m, 0, source).wait_recv()
            total = total + stat[m, source]
        col[m, me] = total / depth
        return begun([
            remote(col.at[m, me], col.at[m, me], col_send.at[m, d], col_recv.at[m, d], {"shard": shifted(d)})
            for d in range(1, n)
        ])

    def block_copy(m, k, first, count, source):
        return remote(
            wbuf.at[m, k, pl.ds(first, count)],
            lands[m].at[pl.ds(pl.multiple_of(source * rows + first, 16), count)],
            send_sem.at[m, k], recv_sem.at[m, source], {"shard": target(k)},
        )

    mixed = interleaved(half, own)

    def ready(m, start, stop):
        def chunk(i, carry):
            first = pl.multiple_of(i * CHUNK, CHUNK)
            at = pl.ds(first, CHUNK)
            behind = None
            for k in mixed + [own]:
                latest = merged(block(m, k)[at, :], lbuf[m, at, :], hbuf[m, k])
                narrow = (latest / col[m, target(k)]).astype(jnp.bfloat16)
                if m < 2 and k == own:
                    lands[m][pl.ds(pl.multiple_of(me * rows + first, CHUNK), CHUNK), :] = narrow
                else:
                    block(m, k)[at, :] = narrow
                if m < 2 and behind is not None:
                    block_copy(m, behind, first, CHUNK, me).start()
                behind = k
            return carry

        lax.fori_loop(start, stop, chunk, 0)

    def extra_copy(k, here, first, count):
        return remote(
            later.at[k, pl.ds(first, count)], head.at[here, pl.ds(first, count)],
            extra_send.at[k], extra_recv.at[here], {"shard": target(k)},
        )

    chunks = rows // CHUNK
    early = chunks // 4
    send_raw(0)
    sums(0)
    send_raw(1)
    fetch(1)
    scales = columns(0)
    send_raw(2)
    begun([raw_low(k, place) for k in range(half)])
    settle(scales)
    ready(0, 0, early)
    settle(gain_loads)
    norm[me, side, 0, :] = gains[0] + gains[1]
    sums(1)
    fetch(2)
    norms = begun([
        remote(norm.at[me, side], norm.at[me, side], norm_send.at[d], norm_recv.at[d], {"shard": shifted(d)})
        for d in range(1, n)
    ])
    ready(0, early, 2 * early)
    scales = columns(1)
    sums(2)
    ready(0, 2 * early, 3 * early)
    last = columns(2)
    ready(0, 3 * early, chunks)
    for i in range(half):
        raw_low(0, i).wait_recv()
    mine = pl.ds(pl.multiple_of(side * share, share), share)
    spreads = begun([
        remote(
            rawlow.at[:, mine], rawlow.at[:, mine], spread_send.at[j], spread_recv.at[j],
            {"tp": lax.rem(side + j, parts)},
        )
        for j in range(1, parts)
    ])
    settle(scales)
    ready(1, 0, chunks)
    settle(last)
    ready(2, 0, chunks)

    @pl.when(side % 2 == 1)
    def _():
        def more(i, carry):
            first = pl.multiple_of(i * CHUNK, CHUNK)
            for k in range(half):
                extra_copy(k, place, first, CHUNK).start()
            return carry

        lax.fori_loop(RAW // CHUNK, (RAW + EXTRA) // CHUNK, more, 0)

    settle(norms)
    sides = begun([
        remote(norm.at[:, side], norm.at[:, side], side_send.at[j], side_recv.at[j], {"tp": lax.rem(side + j, parts)})
        for j in range(1, parts)
    ])
    settle(spreads)
    for i in range(half):
        for p in range(len(RAW_PARTS)):
            raw_part(p, 0, i).wait_recv()
        low = jnp.transpose(rawlow[i].astype(jnp.float32)).astype(jnp.bfloat16)
        latest = merged(raw[i], low, hbuf[2, own])
        head[i, pl.ds(0, RAW), :] = (latest / col[2, me]).astype(jnp.bfloat16)
    settle(sides)

    for k in range(half):
        for p in range(len(RAW_PARTS)):
            raw_part(p, k, place).wait_send()
        raw_low(k, place).wait_send()
    for k in range(own):
        for m in range(3):
            part_copy(m, k, me).wait_send()
        for m in range(2):
            block_copy(m, k, 0, rows, me).wait_send()
    for m in range(2):
        for d in range(1, n):
            block_copy(m, 0, 0, rows, shifted(d)).wait_recv()

    @pl.when(side % 2 == 1)
    def _():
        for i in range(half):
            extra_copy(i, place, RAW, EXTRA).wait_send()
            extra_copy(0, i, RAW, EXTRA).wait_recv()


def exchange_value(n, later, _, land, send_sem, recv_sem):
    rows = later.shape[1]
    me, half, top, place, target = places(n)
    parity = lax.axis_index("tp") % 2
    own = n - 1
    barrier = pltpu.get_barrier_semaphore()
    for d in range(1, n):
        pl.semaphore_signal(
            barrier, inc=1, device_id={"shard": lax.rem(me + d, n)}, device_id_type=MESH
        )
    pl.semaphore_wait(barrier, n - 1)

    def block_copy(k, first, count, source):
        return pltpu.make_async_remote_copy(
            src_ref=later.at[k, pl.ds(first, count)],
            dst_ref=land.at[pl.ds(pl.multiple_of(source * rows + first, 16), count)],
            send_sem=send_sem.at[k], recv_sem=recv_sem.at[source],
            device_id={"shard": target(k)}, device_id_type=MESH,
        )

    chunks = rows // CHUNK
    near = list(range(half, own))
    for odd in range(2):
        skip = RAW + odd * EXTRA

        @pl.when(parity == odd)
        def _():
            def both(i, carry):
                first = pl.multiple_of(i * CHUNK, CHUNK)
                for k in interleaved(half, own):
                    block_copy(k, first + skip if k < half else first, CHUNK, me).start()
                return carry

            def rest(i, carry):
                for k in near:
                    block_copy(k, pl.multiple_of(i * CHUNK, CHUNK), CHUNK, me).start()
                return carry

            far = chunks - skip // CHUNK
            lax.fori_loop(0, far, both, 0)
            lax.fori_loop(far, chunks, rest, 0)
            for k in range(own):
                first = skip if k < half else 0
                block_copy(k, first, rows - first, me).wait_send()
            for i in range(half):
                block_copy(0, skip, rows - skip, (1 - top) * half + i).wait_recv()
            for d in range(1, half):
                block_copy(half, 0, rows, top * half + lax.rem(place + d, half)).wait_recv()


def finish(q_in, k_in, col, norm, q_out, k_out, q_col, k_col, v_col, serve, sem):
    step = q_in.shape[0] // PIECES
    copies = [
        pltpu.make_async_copy(source.at[pl.ds(i * step, step)], out.at[pl.ds(i * step, step)], sem.at[m, i])
        for m, (source, out) in enumerate(((q_in, q_out), (k_in, k_out)))
        for i in range(PIECES)
    ]
    for copy in copies:
        copy.start()
    me = lax.axis_index("shard")
    for m, out in enumerate((q_col, k_col, v_col)):
        out[...] = col[m, me, 0, :]
    n, parts, _, piece = norm.shape
    for s in range(n):
        for t in range(parts):
            serve[pl.ds((s * parts + t) * piece, piece)] = norm[s, t, 0, :].astype(jnp.bfloat16)
    for copy in copies:
        copy.wait()


def finish_value(n, land, head, later, out, own_sem, near_sem, head_sem, extra_sem, far_sem):
    rows = later.shape[1]
    me, half, top, place, _ = places(n)
    parity = lax.axis_index("tp") % 2

    def at(source, first, count):
        return pl.ds(pl.multiple_of(source * rows + first, 16), count)

    def moved(source, first, count, sem):
        here = at(source, first, count)
        return pltpu.make_async_copy(land.at[here], out.at[here], sem)

    def kept(i, source, first, count, sem):
        return pltpu.make_async_copy(head.at[i, pl.ds(first, count)], out.at[at(source, first, count)], sem)

    copies = [pltpu.make_async_copy(later.at[n - 1], out.at[at(me, 0, rows)], own_sem)]
    for d in range(1, half):
        copies.append(moved(top * half + lax.rem(place + d, half), 0, rows, near_sem.at[d]))
    split = RAW + EXTRA
    sources = [(1 - top) * half + i for i in range(half)]
    for i, source in enumerate(sources):
        copies.append(kept(i, source, 0, RAW, head_sem.at[i]))
        copies.append(moved(source, split, rows - split, far_sem.at[i]))
    for copy in copies:
        copy.start()

    @pl.when(parity == 0)
    def _():
        for i, source in enumerate(sources):
            moved(source, RAW, EXTRA, extra_sem.at[i]).start()

    @pl.when(parity == 1)
    def _():
        for i, source in enumerate(sources):
            kept(i, source, RAW, EXTRA, extra_sem.at[i]).start()

    for i, source in enumerate(sources):
        copies.append(moved(source, RAW, EXTRA, extra_sem.at[i]))
    for copy in copies:
        copy.wait()


def kernel_body(
    n, parts,
    weight_query, low_query, high_query,
    weight_key, low_key, high_key,
    weight_value, low_value, high_value,
    norm_train, norm_step,
):
    rows, wide = weight_query.shape
    width, depth = wide // n, rows * n
    rank, piece = low_query.shape[1], norm_train.shape[0]
    anywhere = pl.BlockSpec(memory_space=pl.ANY)
    vmem = pl.BlockSpec(memory_space=pltpu.VMEM)
    land = pltpu.VMEM((depth, width), jnp.bfloat16)
    later = pltpu.VMEM((n, rows, width), jnp.bfloat16)
    dma = pltpu.SemaphoreType.DMA
    half = n // 2
    land_q, land_k, value, head, col, norm = pl.pallas_call(
        functools.partial(exchange, n, parts, depth),
        out_shape=(
            land, land, later,
            pltpu.VMEM((half, RAW + EXTRA, width), jnp.bfloat16),
            pltpu.VMEM((3, n, 1, width), jnp.float32),
            pltpu.VMEM((n, parts, 1, piece), jnp.float32),
        ),
        in_specs=[anywhere] * 11,
        out_specs=(vmem,) * 6,
        scratch_shapes=[
            pltpu.VMEM((2, n, rows, width), jnp.bfloat16),
            pltpu.VMEM((3, rank, rows), jnp.bfloat16),
            pltpu.VMEM((3, rows, rank), jnp.bfloat16),
            pltpu.VMEM((3, n, rank, width), jnp.bfloat16),
            pltpu.VMEM((3, n, 1, width), jnp.float32),
            pltpu.VMEM((3, n, 1, width), jnp.float32),
            pltpu.VMEM((half, RAW, width), jnp.bfloat16),
            pltpu.VMEM((half, rank, RAW), jnp.bfloat16),
            pltpu.VMEM((2, piece), jnp.float32),
            dma((3, n)), dma((3, n)), dma((3,)), dma((2,)),
            dma((2, n)), dma((2, n)), dma((3, n)), dma((3, n)), dma((3, n)), dma((3, n)),
            dma((len(RAW_PARTS), half)), dma((len(RAW_PARTS), half)),
            dma((half,)), dma((half,)), dma((parts,)), dma((parts,)),
            dma((n,)), dma((n,)), dma((parts,)), dma((parts,)), dma((half,)), dma((half,)),
        ],
        compiler_params=pltpu.CompilerParams(
            collective_id=0, has_side_effects=True, vmem_limit_bytes=28 * 2**20
        ),
        name="exchange",
    )(
        weight_query, weight_key, weight_value,
        low_query.T, low_key.T, low_value.T,
        high_query, high_key, high_value,
        norm_train, norm_step,
    )
    ready = jax.ShapeDtypeStruct((depth, width), jnp.bfloat16)
    column = jax.ShapeDtypeStruct((width,), jnp.float32)
    ready_q, ready_k, col_q, col_k, col_v, serve = pl.pallas_call(
        finish,
        out_shape=(
            (ready,) * 2 + (column,) * 3
            + (jax.ShapeDtypeStruct((n * parts * piece,), jnp.bfloat16),)
        ),
        in_specs=[anywhere] * 2 + [vmem] * 2,
        out_specs=(anywhere,) * 2 + (vmem,) * 4,
        scratch_shapes=[dma((2, PIECES))],
        compiler_params=pltpu.CompilerParams(vmem_limit_bytes=2**20),
        name="finish",
    )(land_q, land_k, col, norm)
    land_v = pl.pallas_call(
        functools.partial(exchange_value, n),
        out_shape=land,
        in_specs=[vmem, anywhere],
        out_specs=vmem,
        scratch_shapes=[dma((n,)), dma((n,))],
        compiler_params=pltpu.CompilerParams(
            collective_id=1, has_side_effects=True, vmem_limit_bytes=2**20
        ),
        name="exchange_value",
    )(value, col_q)
    ready_v = pl.pallas_call(
        functools.partial(finish_value, n),
        out_shape=ready,
        in_specs=[anywhere] * 3,
        out_specs=anywhere,
        scratch_shapes=[dma(()), dma((half,)), dma((half,)), dma((half,)), dma((half,))],
        compiler_params=pltpu.CompilerParams(vmem_limit_bytes=2**20),
        name="finish_value",
    )(land_v, head, value)
    return (ready_q, ready_k, ready_v, col_q, col_k, col_v, serve)


def plain_body(
    weight_query, low_query, high_query,
    weight_key, low_key, high_key,
    weight_value, low_value, high_value,
    norm_train, norm_step,
):
    n = lax.axis_size("shard")
    latest = [
        merged(weight, low, high)
        for weight, low, high in (
            (weight_query, low_query, high_query),
            (weight_key, low_key, high_key),
            (weight_value, low_value, high_value),
        )
    ]
    totals = lax.psum(tuple(jnp.sum(jnp.abs(x), axis=0) for x in latest), "shard")
    place = lax.axis_index("shard")
    readies, columns = [], []
    for x, total in zip(latest, totals):
        column = total / (x.shape[0] * n)
        narrow = (x / column).astype(jnp.bfloat16)
        ready = lax.all_to_all(narrow, "shard", split_axis=1, concat_axis=0, tiled=True)
        readies.append(ready)
        columns.append(lax.dynamic_slice_in_dim(column, place * ready.shape[1], ready.shape[1]))
    serve = (norm_train + norm_step).astype(jnp.bfloat16)
    serve = lax.all_gather(serve, ("shard", "tp"), tiled=True)
    return (*readies, *columns, serve)


def solution(mesh):
    n, parts = mesh.shape["shard"], mesh.shape["tp"]

    def body(*args):
        rows, wide = args[0].shape
        fits = (
            n % 4 == 0
            and wide % (n * 128) == 0
            and rows % TILE == 0
            and rows % (4 * CHUNK) == 0
            and rows > RAW + EXTRA
            and args[1].shape[1] % (16 * parts) == 0
            and rows * n % PIECES == 0
            and all(args[i].shape == args[0].shape for i in (3, 6))
            and 6 * rows * wide < 40 * 2**20
        )
        if fits:
            return kernel_body(n, parts, *args)
        return plain_body(*args)

    weight, low, high = P("shard", "tp"), P("shard", None), P(None, "tp")
    norm = P(("shard", "tp"))
    ready, column = P(None, ("tp", "shard")), P(("tp", "shard"))
    return jax.shard_map(
        body,
        mesh=mesh,
        in_specs=(weight, low, high) * 3 + (norm, norm),
        out_specs=(ready,) * 3 + (column,) * 3 + (P(),),
        check_vma=False,
    )
```

time: 632 us -> 621 us (0.983)
  Pallas kernels: 628 us -> 616 us
    pallas_call x1, Pallas kernels: 617 us -> 462 us  [kernel_body(): pl.pallas_call(functools.partial(exchange, n, parts, depth), out_shape=(l...]
    pallas_call x1 -> x3, Pallas kernels: 10.3 us -> 154 us  [the longest x1 143 us: kernel_body(): pl.pallas_call(functools.partial(exchange_value, n), out_shape=land, in_s...]
where the time goes in v1:
time: 621 us; the launch traced here: 617 us
  Pallas kernels  616 us (99%)
    pallas_call x1, Pallas kernels, kernel_body(): pl.pallas_call(functools.partial(exchange, n, parts, depth), out_shape=(l...  462 us
    pallas_call x1, Pallas kernels, kernel_body(): pl.pallas_call(functools.partial(exchange_value, n), out_shape=land, in_s...  143 us

profile of v1, /device:TPU:30, one launch (start us, length us, event | category | flops | bytes accessed | tf_op | source)
XLA Modules:
  0.0 617.1 jit_solution(7525409261369341531)
XLA Ops:
  0.6 462.0 %exchange.1 = (bf16[12288,384]{1,0:T(8,128)(2,1)S(1)}, bf16[12288,384]{1,0:T(8,128)(2,1)S(1)}, bf16[8,1536,384]{2,1,0:T(8,128)(2,1)S(1)}, bf16[4,768,384]{2,1,0:...) custom-call(bf16[1536,3072]{1,0:T(8,128)(2,1)} %wq.1, bf16[1536,3072]{1,0:T(8,128)(2,1)} %wk.1, ...), custom_call_target="tpu_custom_call" | custom-call | tf_op jit(solution)/shard_map/exchange/pallas_call | solution.py:422
  462.6 7.2 %finish.1 = (bf16[12288,384]{1,0:T(8,128)(2,1)}, bf16[12288,384]{1,0:T(8,128)(2,1)}, f32[384]{0:T(512)}, f32[384]{0:T(512)}, f32[384]{0:T(512)}, /*index=5*/bf16[12288]{0:T(1024)(128)(2,1)}) custom-call(bf16[12288,384]{1,0:T(8,128)(2,1)S(1)} %get-tuple-element.19.q_in, bf16[12288,384]{1,0:T(8,128)(2,1)S(1)} %get-tuple-element.20.k_in, ...), custom_call_target="tpu_custom_call" | custom-call | tf_op jit(solution)/shard_map/finish/pallas_call | solution.py:460
  469.8 0.0 copy-start
  469.8 0.7 copy-done
  470.5 142.8 %exchange_value.1.land = bf16[12288,384]{1,0:T(8,128)(2,1)S(1)} custom-call(bf16[8,1536,384]{2,1,0:T(8,128)(2,1)S(1)} %get-tuple-element.25.later, f32[384]{0:T(512)S(1)} %copy-done), custom_call_target="tpu_custom_call" | custom-call | tf_op jit(solution)/shard_map/exchange_value/pallas_call | solution.py:472
  613.3 3.8 finish_value.1
Async XLA Ops:
  469.8 0.7 copy-start
